TPU v7x, 32 devices: a whole 2x2x4 slice. The times are simulated.
32 devices in a mesh: rep: 8 (over y, x, core), shard: 4 (over z).
Axes of the slice: x: 2, y: 2, z: 4, core: 2. Of those that a mesh axis runs over, the one named last changes fastest.
Arguments:
- activations: bfloat16 [6, 4096, 2048], P(None, ('rep', 'shard')), may hold values from -50 to 50
- cotangents: bfloat16 [6, 4096, 512], P(None, ('rep', 'shard')), may hold values from -120 to 120
- momentum: float32 [12, 256, 2048], P(None, None, 'shard'), may hold values from -6 to 6
- owners: int32 [12], replicated, may hold values from 0 to 3, as said below
- bucket_starts: int32 [2], replicated, may hold values from 1 to 11, as said below
Outputs:
- momentum_out: float32 [12, 256, 2048], P(None, None, 'shard')
- update: float32 [12, 256, 2048], P(None, None, 'shard')
- owned: bfloat16 [16, 256, 2048], P('shard')
Inputs may be any that keep to these rules, and one draw needn't show every extreme that they name: `owners`: no owner is named more than 4 times, and some owner exactly 4 times. `bucket_starts`: strictly increasing.
All inputs are finite; a program needn't handle non-finite values.
Results may differ from a plain program's by a relative error of at most 0.033.
Values may be sent and summed in bfloat16 or wider, within the bound.
No kernel may reach another device: no remote copies, remote signals or barrier semaphores. Data moves between devices by JAX's collectives and lax.ppermute only.
A program may use at most 128 MiB of HBM per device.

v0:
```python
import math
import jax
import jax.numpy as jnp
from jax import lax
from jax.sharding import PartitionSpec as P

D = 2048
KV = 256
ITERS = 5
MATS = 12
coef_a = 3.4445
coef_b = -4.775
coef_c = 2.0315
momentum_rate = 0.95
clip_level = 0.5
epsilon = 1e-06


def orthogonal_batch(matrices):
    values = matrices.astype(jnp.float32)
    frobenius = jnp.sqrt(jnp.sum(values * values, axis=(1, 2), keepdims=True))
    matrix = (values / (frobenius + epsilon)).astype(jnp.bfloat16)
    for iteration in range(ITERS):
        gram_matrix = jnp.einsum(
            "skd,sjd->skj", matrix, matrix, preferred_element_type=jnp.float32
        ).astype(jnp.bfloat16)
        square = jnp.einsum(
            "skj,sji->ski", gram_matrix, gram_matrix, preferred_element_type=jnp.float32
        )
        mixing = (coef_b * gram_matrix.astype(jnp.float32) + coef_c * square).astype(jnp.bfloat16)
        product = jnp.einsum("skj,sjd->skd", mixing, matrix, preferred_element_type=jnp.float32)
        matrix = (coef_a * matrix.astype(jnp.float32) + product).astype(jnp.bfloat16)
    return matrix


def clip_factors(square_sums, bucket_starts):
    indices = jnp.arange(MATS, dtype=jnp.int32)
    buckets = jnp.sum((indices[:, None] >= bucket_starts[None, :]).astype(jnp.int32), axis=1)
    together = (buckets[:, None] == buckets[None, :]).astype(jnp.float32)
    totals = jnp.sum(together * square_sums[None, :], axis=1)
    members = jnp.sum(together, axis=1)
    root_mean = jnp.sqrt(totals / (members * KV * D) + epsilon)
    return jnp.minimum(1.0, clip_level / root_mean)


def slot_numbers(owners):
    indices = jnp.arange(MATS, dtype=jnp.int32)
    earlier = (indices[None, :] < indices[:, None]) & (owners[None, :] == owners[:, None])
    return jnp.sum(earlier.astype(jnp.int32), axis=1)


def selector(owner_of, slot_of, shard_count, slot_count):
    holders = lax.broadcasted_iota(jnp.int32, (shard_count, slot_count, 1), 0)
    places = lax.broadcasted_iota(jnp.int32, (shard_count, slot_count, 1), 1)
    chosen = (holders == owner_of[None, None, :]) & (places == slot_of[None, None, :])
    return chosen.astype(jnp.bfloat16)


def pack_slots(shards, chooser):
    return jnp.einsum("psm,mkd->skpd", chooser, shards, preferred_element_type=jnp.float32).astype(
        jnp.bfloat16
    )


def unpack_slots(received, chooser):
    return jnp.einsum("psm,skpd->mkd", chooser, received, preferred_element_type=jnp.float32)


def per_device(activations, cotangents, momentum, owners, bucket_starts):
    shard_count = lax.axis_size("shard")
    replica_count = lax.axis_size("rep")
    layers, tok_rows, width = activations.shape
    token_total = tok_rows * shard_count * replica_count
    columns = width // shard_count
    slot_count = -(-MATS // shard_count) + 1
    update_scale = math.sqrt(max(KV, D))
    partial_terms = jnp.einsum(
        "ltk,ltd->lkd", cotangents, activations, preferred_element_type=jnp.float32
    ).reshape(MATS, KV, width)
    shard_part = lax.psum_scatter(
        partial_terms.astype(jnp.bfloat16), "shard", scatter_dimension=2, tiled=True
    )
    summed = lax.psum(shard_part, "rep").astype(jnp.float32)
    gradient = summed / jnp.sqrt(jnp.float32(token_total))
    square_sums = lax.psum(jnp.sum(gradient * gradient, axis=(1, 2)), "shard")
    factors = clip_factors(square_sums, bucket_starts)
    momentum_out = momentum_rate * momentum + factors[:, None, None] * gradient
    nesterov = (factors[:, None, None] * gradient + momentum_rate * momentum_out).astype(
        jnp.bfloat16
    )
    slot_of = slot_numbers(owners)
    chooser = selector(owners, slot_of, shard_count, slot_count)
    received = lax.all_to_all(
        pack_slots(nesterov, chooser), "shard", split_axis=2, concat_axis=2, tiled=True
    )
    item_count = received.shape[0]
    result = orthogonal_batch(received.reshape(item_count, KV, width))
    scaled = (update_scale * result.astype(jnp.float32)).astype(jnp.bfloat16)
    returned_part = lax.all_to_all(
        result.reshape(item_count, KV, shard_count, columns),
        "shard",
        split_axis=2,
        concat_axis=2,
        tiled=True,
    )
    update = update_scale * unpack_slots(returned_part, chooser)
    return (momentum_out, update, scaled)


def solution(mesh):
    placed = (
        P(None, ("rep", "shard"), None),
        P(None, ("rep", "shard"), None),
        P(None, None, "shard"),
        P(),
        P(),
    )
    return jax.shard_map(
        per_device,
        mesh=mesh,
        in_specs=placed,
        out_specs=(P(None, None, "shard"), P(None, None, "shard"), P("shard", None, None)),
        check_vma=False,
    )
```

profile of v0, /device:TPU:0, one launch (start us, length us, event | category | flops | bytes accessed | tf_op | source)
XLA Modules:
  0.0 628.7 jit_solution(7850183555704222649)
XLA Ops:
  9.1 7.5 %convolution_convert_fusion = bf16[6,512,2048]{2,1,0:T(8,128)(2,1)} fusion(bf16[6,128,512]{2,1,0:T(8,128)(2,1)} %param.6, bf16[6,128,2048]{2,1,0:T(8,128)(2,1)S(1)} %copy-done), kind=kOutput, calls=%fused_computation.13 | convolution fusion | flops 1616904192 | bytes 16515072 | tf_op jit(solution)/shard_map/ltk,ltd->lkd/dot_general | solution.py:77
  16.7 214.7 %reduce-scatter.2.cloned.1.call-done = bf16[12,256,512]{2,1,0:T(8,128)(2,1)} async-done(((bf16[12,256,2048]{2,1,0:T(8,128)(2,1)}), bf16[12,256,512]{2,1,0:T(8,128)(2,1)}) %reduce-scatter.2.cloned.1.call-update) | async-done | bytes 3145744 | tf_op jit(solution)/shard_map/reduce_scatter | solution.py:80
  231.6 73.4 %all-reduce.2.cloned.1.call-done = bf16[12,256,512]{2,1,0:T(8,128)(2,1)} async-done(((bf16[12,256,512]{2,1,0:T(8,128)(2,1)}), bf16[12,256,512]{2,1,0:T(8,128)(2,1)}) %all-reduce.2.cloned.1.call-update) | async-done | bytes 3145744 | tf_op jit(solution)/shard_map/psum | solution.py:83
  308.0 11.7 %psum.15 = f32[12]{0:T(128)S(1)} all-reduce(f32[12]{0:T(128)S(1)} %fusion.4), channel_id=1, replica_groups=mesh['rep'=8,'shard'=4] {'shard'}, use_global_device_ids=true, to_apply=%region_4.0 | all-reduce | flops 12 | bytes 96 | tf_op jit(solution)/shard_map/psum | solution.py:85
  319.9 8.1 %fusion.9 = (bf16[12,256,512,1]{2,1,0,3:T(8,128)(2,1)S(1)}, f32[12,256,512]{2,1,0:T(8,128)}) fusion(bf16[12,256,512]{2,1,0:T(8,128)(2,1)} %all-reduce.2.cloned.1.call-done, f32[12]{0:T(128)S(1)} %minimum_multiply_fusion, f32[12,256,512]{2,1,0:T(8,128)} %param.7), kind=kLoop, calls=%fused_computation.20 | loop fusion | flops 11010048 | bytes 18874416 | tf_op jit(solution)/shard_map/convert_element_type | solution.py:88
  332.2 94.6 %all_to_all.10 = bf16[4,256,4,512]{3,0,1,2:T(4,128)(2,1)} all-to-all(bf16[4,256,4,512]{3,0,1,2:T(4,128)(2,1)S(1)} %copy.28), channel_id=1, replica_groups=mesh['rep'=8,'shard'=4] {'shard'}, dimensions={2} | all-to-all | bytes 8388608 | tf_op jit(solution)/shard_map/all_to_all | solution.py:93
  426.8 7.5 %copy.29 = bf16[4,256,4,512]{1,3,2,0:T(8,128)(2,1)} copy(bf16[4,256,4,512]{3,0,1,2:T(4,128)(2,1)} %all_to_all.10) | data formatting | bytes 8388608 | tf_op jit(solution)/shard_map/all_to_all | solution.py:93
  434.3 3.4 multiply_reduce_fusion
  437.6 6.9 %copy.30 = f32[4,256,2048]{2,1,0:T(8,128)} copy(bf16[4,256,2048]{1,2,0:T(8,128)(2,1)} %bitcast.48) | data formatting | bytes 12582912 | tf_op jit(solution)/shard_map/convert_element_type | solution.py:20
  444.6 4.6 divide_convert_fusion
  452.5 6.3 add_convert_fusion.4
  458.7 4.7 convolution_convert_fusion.5
  463.5 6.3 add_convert_fusion.3
  469.7 4.8 convolution_convert_fusion.4
  474.5 6.3 add_convert_fusion.2
  480.8 4.7 convolution_convert_fusion.3
  485.5 6.3 add_convert_fusion.1
  491.8 4.7 convolution_convert_fusion.2
  496.6 7.7 %multiply_convert_fusion = (bf16[4,256,2048]{2,1,0:T(8,128)(2,1)}, bf16[4,256,2048]{2,1,0:T(8,128)(2,1)}) fusion(bf16[4,256,2048]{2,1,0:T(8,128)(2,1)} %add_convert_fusion.1, bf16[4,256,256]{2,1,0:T(8,128)(2,1)S(1)} %convolution_convert_fusion.2), kind=kOutput, calls=%fused_computation.1 | convolution fusion | flops 1223950336 | bytes 13107200 | tf_op jit(solution)/shard_map/skj,sjd->skd/dot_general | solution.py:31
  504.3 7.8 %reshape.38 = bf16[4,256,4,512]{3,2,1,0:T(4,128)(2,1)} reshape(bf16[4,256,2048]{2,1,0:T(8,128)(2,1)} %get-tuple-element.20) | data formatting | bytes 8388608 | tf_op jit(solution)/shard_map/reshape | solution.py:100
  512.1 5.4 copy.31
  517.5 94.6 %all_to_all.11 = bf16[4,256,4,512]{3,0,1,2:T(4,128)(2,1)S(1)} all-to-all(bf16[4,256,4,512]{3,0,1,2:T(4,128)(2,1)S(1)} %copy.31), channel_id=1, replica_groups=mesh['rep'=8,'shard'=4] {'shard'}, dimensions={2} | all-to-all | bytes 8388608 | tf_op jit(solution)/shard_map/all_to_all | solution.py:99
  612.2 3.4 bitcast_multiply_fusion
  615.5 6.3 %copy.33 = f32[12,256,512]{2,1,0:T(8,128)} copy(f32[12,256,512]{2,0,1:T(8,128)S(1)} %bitcast_multiply_fusion) | data formatting | bytes 12582912
  (23 shorter events, 12.8 us)
Async XLA Ops:
  7.2 1.9 copy-start
  7.2 224.2 %reduce-scatter.2.cloned.1.call-start = ((), (), s32[]{:S(2)}) async-start(), calls=%async_computation.3 | async-start | bytes 15728640 | tf_op jit(solution)/shard_map/reduce_scatter | solution.py:80
  16.6 214.8 %copy-start.3 = (s32[12]{0:T(128)S(1)}, s32[12]{0:T(128)}, u32[]{:S(2)}) copy-start(s32[12]{0:T(128)} %param.8) | copy-start | bytes 148
  16.6 291.3 %copy-start.4 = (s32[2]{0:T(128)S(1)}, s32[2]{0:T(128)}, u32[]{:S(2)}) copy-start(s32[2]{0:T(128)} %param.9) | copy-start | bytes 28
  16.6 288.4 %all-reduce.2.cloned.1.call-start = ((), (), s32[]{:S(2)}) async-start(), calls=%async_computation.4 | async-start | bytes 6291456 | tf_op jit(solution)/shard_map/psum | solution.py:83
  449.2 2.0 copy-start.2
  612.2 9.7 %copy-start.1 = (bf16[6,128,2048]{2,1,0:T(8,128)(2,1)S(1)}, bf16[6,128,2048]{2,1,0:T(8,128)(2,1)}, u32[]{:S(2)}) copy-start(bf16[6,128,2048]{2,1,0:T(8,128)(2,1)} %param.5) | copy-start | bytes 9437188
Sparse Core Ops, SparseCore 0:
  16.7 214.6 reduce-scatter.1
  234.7 70.3 all-reduce.1
where the time goes:
time: 630 us; the launch traced here: 629 us
  waiting for transfers between devices  288 us (46%)
  blocking collectives  201 us (32%)
  matrix products  66.7 us (11%)
  local copies, waits for them, and re-layouts  39.3 us (6%)
  other arithmetic  19.4 us (3%)
  between operations  14.1 us (2%)
    reduce_scatter x1, waiting for transfers between devices, per_device(): lax.psum_scatter(partial_terms.astype(jnp.bfloat16), 'shard', scatter_dim...  215 us
    all_to_all x1, blocking collectives, per_device(): lax.all_to_all(result.reshape(item_count, KV, shard_count, columns), 'sha...  94.6 us
    all_to_all x1, blocking collectives, per_device(): lax.all_to_all(pack_slots(nesterov, chooser), 'shard', split_axis=2, conc...  94.6 us
    psum x1, waiting for transfers between devices, per_device(): summed = lax.psum(shard_part, 'rep').astype(jnp.float32)  73.4 us
    dot_general x5, matrix products, orthogonal_batch(): jnp.einsum('skj,sjd->skd', mixing, matrix, preferred_element_type=jnp.flo...  32.7 us
    dot_general x5, matrix products, orthogonal_batch(): jnp.einsum('skd,sjd->skj', matrix, matrix, preferred_element_type=jnp.flo...  20.3 us
    reshape x2, local copies, waits for them, and re-layouts, per_device(): result.reshape(item_count, KV, shard_count, columns)  13.2 us
  transfers between devices with their start and end apart: 2, of which 2 were waited for; matrix products, arithmetic and copies ran while one was open for 0% of the time, Pallas kernels for 0%

commit v1 on v0

--- a/solution.py
+++ b/solution.py
@@ -90,8 +90,14 @@
     )
     slot_of = slot_numbers(owners)
     chooser = selector(owners, slot_of, shard_count, slot_count)
-    received = lax.all_to_all(
-        pack_slots(nesterov, chooser), "shard", split_axis=2, concat_axis=2, tiled=True
+    received = jnp.concatenate(
+        lax.all_to_all(
+            jnp.stack(jnp.split(pack_slots(nesterov, chooser), lax.axis_size("shard"), axis=2)),
+            "shard",
+            0,
+            0,
+        ),
+        axis=2,
     )
     item_count = received.shape[0]
     result = orthogonal_batch(received.reshape(item_count, KV, width))

time: 630 us -> 651 us (1.033)
  other arithmetic: 19.4 us -> 28.8 us
    convert_element_type x1 -> x2, local copies, waits for them, and re-layouts: 6.94 us -> 18.6 us  [orthogonal_batch(): values = matrices.astype(jnp.float32)]
    all_to_all x1 -> x0, local copies, waits for them, and re-layouts: 7.45 us -> none  [per_device(): lax.all_to_all(pack_slots(nesterov, chooser), 'shard', split_axis=2, conc...]
where the time goes in v1:
time: 651 us; the launch traced here: 643 us
  waiting for transfers between devices  288 us (44%)
  blocking collectives  201 us (31%)
  matrix products  66.9 us (10%)
  local copies, waits for them, and re-layouts  44.2 us (7%)
  other arithmetic  28.8 us (4%)
  between operations  14.4 us (2%)
    reduce_scatter x1, waiting for transfers between devices, per_device(): lax.psum_scatter(partial_terms.astype(jnp.bfloat16), 'shard', scatter_dim...  215 us
    all_to_all x1, blocking collectives, per_device(): lax.all_to_all(result.reshape(item_count, KV, shard_count, columns), 'sha...  94.9 us
    all_to_all x1, blocking collectives, per_device(): lax.all_to_all(jnp.stack(jnp.split(pack_slots(nesterov, chooser), lax.axi...  94.2 us
    psum x1, waiting for transfers between devices, per_device(): summed = lax.psum(shard_part, 'rep').astype(jnp.float32)  73.4 us
    dot_general x5, matrix products, orthogonal_batch(): jnp.einsum('skj,sjd->skd', mixing, matrix, preferred_element_type=jnp.flo...  32.9 us
    dot_general x5, matrix products, orthogonal_batch(): jnp.einsum('skd,sjd->skj', matrix, matrix, preferred_element_type=jnp.flo...  20.3 us
    convert_element_type x2, local copies, waits for them, and re-layouts, orthogonal_batch(): values = matrices.astype(jnp.float32)  18.6 us
    reshape x2, local copies, waits for them, and re-layouts, per_device(): result.reshape(item_count, KV, shard_count, columns)  13.2 us
  transfers between devices with their start and end apart: 2, of which 2 were waited for; matrix products, arithmetic and copies ran while one was open for 0% of the time, Pallas kernels for 0%

profile of v1, /device:TPU:0, one launch (start us, length us, event | category | flops | bytes accessed | tf_op | source)
XLA Modules:
  0.0 643.3 jit_solution(724655441479620508)
XLA Ops:
  9.1 7.5 %convolution_convert_fusion = bf16[6,512,2048]{2,1,0:T(8,128)(2,1)} fusion(bf16[6,128,512]{2,1,0:T(8,128)(2,1)} %param.6, bf16[6,128,2048]{2,1,0:T(8,128)(2,1)S(1)} %copy-done), kind=kOutput, calls=%fused_computation.15 | convolution fusion | flops 1616904192 | bytes 16515072 | tf_op jit(solution)/shard_map/ltk,ltd->lkd/dot_general | solution.py:77
  16.7 214.7 %reduce-scatter.2.cloned.1.call-done = bf16[12,256,512]{2,1,0:T(8,128)(2,1)} async-done(((bf16[12,256,2048]{2,1,0:T(8,128)(2,1)}), bf16[12,256,512]{2,1,0:T(8,128)(2,1)}) %reduce-scatter.2.cloned.1.call-update) | async-done | bytes 3145744 | tf_op jit(solution)/shard_map/reduce_scatter | solution.py:80
  231.6 73.4 %all-reduce.2.cloned.1.call-done = bf16[12,256,512]{2,1,0:T(8,128)(2,1)} async-done(((bf16[12,256,512]{2,1,0:T(8,128)(2,1)}), bf16[12,256,512]{2,1,0:T(8,128)(2,1)}) %all-reduce.2.cloned.1.call-update) | async-done | bytes 3145744 | tf_op jit(solution)/shard_map/psum | solution.py:83
  308.0 11.7 %psum.15 = f32[12]{0:T(128)S(1)} all-reduce(f32[12]{0:T(128)S(1)} %fusion.5), channel_id=1, replica_groups=mesh['rep'=8,'shard'=4] {'shard'}, use_global_device_ids=true, to_apply=%region_4.0 | all-reduce | flops 12 | bytes 96 | tf_op jit(solution)/shard_map/psum | solution.py:85
  319.9 8.1 %fusion.10 = (bf16[12,256,512,1]{2,1,0,3:T(8,128)(2,1)S(1)}, f32[12,256,512]{2,1,0:T(8,128)}) fusion(bf16[12,256,512]{2,1,0:T(8,128)(2,1)} %all-reduce.2.cloned.1.call-done, f32[12]{0:T(128)S(1)} %minimum_multiply_fusion, f32[12,256,512]{2,1,0:T(8,128)} %param.7), kind=kLoop, calls=%fused_computation.23 | loop fusion | flops 11010048 | bytes 18874416 | tf_op jit(solution)/shard_map/convert_element_type | solution.py:88
  336.8 94.2 %all_to_all.10 = bf16[4,4,256,1,512]{4,1,2,3,0:T(4,128)(2,1)S(1)} all-to-all(bf16[4,4,256,1,512]{4,1,2,3,0:T(4,128)(2,1)S(1)} %pad_maximum_fusion), channel_id=1, replica_groups=mesh['rep'=8,'shard'=4] {'shard'}, dimensions={0} | all-to-all | bytes 8388608 | tf_op jit(solution)/shard_map/all_to_all | solution.py:94
  431.0 4.4 fusion
  435.4 4.5 convert_bitcast_fusion
  440.0 9.9 %copy.39 = f32[4,256,4,1,512]{1,4,2,0,3:T(8,128)} copy(f32[4,256,4,1,512]{4,0,1,3,2:T(4,128)} %convert_bitcast_fusion) | data formatting | bytes 16777216 | tf_op jit(solution)/shard_map/convert_element_type | solution.py:20
  449.9 8.7 %copy.40 = f32[4,256,2048]{2,1,0:T(8,128)} copy(f32[4,256,2048]{1,2,0:T(8,128)} %bitcast.63) | data formatting | bytes 16777216 | tf_op jit(solution)/shard_map/convert_element_type | solution.py:20
  458.6 4.6 divide_convert_fusion
  466.5 6.3 add_convert_fusion.4
  472.7 4.7 convolution_convert_fusion.5
  477.5 6.4 add_convert_fusion.3
  483.9 4.8 convolution_convert_fusion.4
  488.7 6.3 add_convert_fusion.2
  495.0 4.7 convolution_convert_fusion.3
  499.7 6.3 add_convert_fusion.1
  506.0 4.7 convolution_convert_fusion.2
  510.7 7.7 %multiply_convert_fusion = (bf16[4,256,2048]{2,1,0:T(8,128)(2,1)}, bf16[4,256,2048]{2,1,0:T(8,128)(2,1)}) fusion(bf16[4,256,2048]{2,1,0:T(8,128)(2,1)} %add_convert_fusion.1, bf16[4,256,256]{2,1,0:T(8,128)(2,1)S(1)} %convolution_convert_fusion.2), kind=kOutput, calls=%fused_computation.4 | convolution fusion | flops 1223950336 | bytes 13107200 | tf_op jit(solution)/shard_map/skj,sjd->skd/dot_general | solution.py:31
  518.4 7.8 %reshape.38 = bf16[4,256,4,512]{3,2,1,0:T(4,128)(2,1)} reshape(bf16[4,256,2048]{2,1,0:T(8,128)(2,1)} %get-tuple-element.24) | data formatting | bytes 8388608 | tf_op jit(solution)/shard_map/reshape | solution.py:106
  526.2 5.4 copy.41
  531.7 94.9 %all_to_all.11 = bf16[4,256,4,512]{3,0,1,2:T(4,128)(2,1)S(1)} all-to-all(bf16[4,256,4,512]{3,0,1,2:T(4,128)(2,1)S(1)} %copy.41), channel_id=1, replica_groups=mesh['rep'=8,'shard'=4] {'shard'}, dimensions={2} | all-to-all | bytes 8388608 | tf_op jit(solution)/shard_map/all_to_all | solution.py:105
  629.9 6.3 copy.43
  (25 shorter events, 20.8 us)
Async XLA Ops:
  7.2 1.9 copy-start
  7.2 224.2 %reduce-scatter.2.cloned.1.call-start = ((), (), s32[]{:S(2)}) async-start(), calls=%async_computation.3 | async-start | bytes 15728640 | tf_op jit(solution)/shard_map/reduce_scatter | solution.py:80
  16.6 214.8 %copy-start.3 = (s32[12]{0:T(128)S(1)}, s32[12]{0:T(128)}, u32[]{:S(2)}) copy-start(s32[12]{0:T(128)} %param.8) | copy-start | bytes 148
  16.6 291.3 %copy-start.4 = (s32[2]{0:T(128)S(1)}, s32[2]{0:T(128)}, u32[]{:S(2)}) copy-start(s32[2]{0:T(128)} %param.9) | copy-start | bytes 28
  16.6 288.4 %all-reduce.2.cloned.1.call-start = ((), (), s32[]{:S(2)}) async-start(), calls=%async_computation.4 | async-start | bytes 6291456 | tf_op jit(solution)/shard_map/psum | solution.py:83
  463.2 2.0 copy-start.2
  626.5 9.7 %copy-start.1 = (bf16[6,128,2048]{2,1,0:T(8,128)(2,1)S(1)}, bf16[6,128,2048]{2,1,0:T(8,128)(2,1)}, u32[]{:S(2)}) copy-start(bf16[6,128,2048]{2,1,0:T(8,128)(2,1)} %param.5) | copy-start | bytes 9437188
Sparse Core Ops, SparseCore 0:
  16.7 214.6 reduce-scatter.1
  234.7 70.3 all-reduce.1
